TPU v7x, 128 devices: a whole 4x4x4 slice. The times are simulated.
128 devices in a mesh: row: 4 (over z), col: 32 (over y, x, core).
Axes of the slice: x: 4, y: 4, z: 4, core: 2. Of those that a mesh axis runs over, the one named last changes fastest.
Arguments:
- eigvecs: float32 [16384, 8192], P('row', 'col'), may hold values from -6 to 6
- v_panels: float32 [8, 16384, 256], P(None, 'row', 'col'), as said below
- t_panels: float32 [8, 256, 256], P(None, None, 'col'), as said below
Outputs:
- rotated: float32 [16384, 8192], P('row', 'col')
Inputs may be any that keep to these rules, and one draw needn't show every extreme that they name: `v_panels`: in panel k, vector j is zero in rows above k * 256 + j + 1, equals 1 in that row and is dense below it. t_panels[k] is upper triangular and V_k t_panels[k] V_k^T = I minus the product of the panel's 256 Householder reflections, each I - 2 v v^T / (v^T v), taken in the order of j; its diagonal lies in (0, 2].
All inputs are finite; a program needn't handle non-finite values.
Results may differ from a plain program's by a relative error of at most 0.00015.
Values sent between devices are 32-bit elements; how exact they have to be, the bound alone decides.
A program may use at most 128 MiB of HBM per device.

v0:
```python
import jax
import jax.numpy as jnp
from jax import lax
from jax.sharding import PartitionSpec as P

exact_precision = lax.Precision.HIGHEST


def gather_turned(arrays, axis, dims):
    turned = [jnp.moveaxis(a, dim, 0) for a, dim in zip(arrays, dims)]
    both = jnp.concatenate([t.reshape(len(t), -1) for t in turned], axis=1)
    result, at, done = (lax.all_gather(both, axis, axis=0, tiled=True), 0, [])
    for t, dim in zip(turned, dims):
        piece = result[:, at : at + t[0].size].reshape(-1, *t.shape[1:])
        done.append(jnp.moveaxis(piece, 0, dim))
        at += t[0].size
    return tuple(done)


def copy_for_each(x, axis):
    length = lax.axis_size(axis)
    return lax.all_to_all(jnp.broadcast_to(x[None], (length, *x.shape)), axis, 0, 0, tiled=True)


def taken_together(x, axis):
    return copy_for_each(x, axis).sum(axis=0)


def matmul(left, right):
    return jnp.dot(left, right, preferred_element_type=jnp.float32, precision=exact_precision)


def project(left, right):
    return lax.dot_general(
        left,
        right,
        (((0,), (0,)), ((), ())),
        precision=exact_precision,
        preferred_element_type=jnp.float32,
    )


def local(eigvecs, v_panels, t_panels):
    panels_total = v_panels.shape[0]
    current = eigvecs
    for panel_index in reversed(range(panels_total)):
        vectors, factor = gather_turned(
            (v_panels[panel_index], t_panels[panel_index]), "col", (1, 1)
        )
        projected = taken_together(project(vectors, current), "row")
        current = current - matmul(vectors, matmul(factor, projected))
    return current


def solution(mesh):
    in_specs = (P("row", "col"), P(None, "row", "col"), P(None, None, "col"))
    out_specs = P("row", "col")
    return jax.shard_map(local, mesh=mesh, in_specs=in_specs, out_specs=out_specs, check_vma=False)
```

profile of v0, /device:TPU:0, one launch (start us, length us, event | category | flops | bytes accessed | tf_op | source)
XLA Modules:
  0.0 441.0 jit_solution(1533209166702690424)
XLA Ops:
  13.9 44.4 %all-gather.9.cloned.1.call-done = f32[256,4352]{1,0:T(8,128)} async-done(((f32[8,4352]{1,0:T(8,128)}), f32[256,4352]{1,0:T(8,128)}) %all-gather.9.cloned.1.call-update) | async-done | bytes 4456464 | tf_op jit(solution)/shard_map/all_gather | solution.py:12
  58.3 7.0 %fusion.22 = f32[256,256]{1,0:T(8,128)S(1)} fusion(f32[4096,256]{1,0:T(8,128)} %param.3, f32[256,4352]{1,0:T(8,128)} %all-gather.9.cloned.1.call-done), kind=kOutput, calls=%fused_computation.30 | convolution fusion | flops 3221225472 | bytes 8650752 | tf_op jit(solution)/shard_map/dot_general | solution.py:34
  65.4 20.0 %all_to_all.40 = f32[4,256,256]{2,1,0:T(8,128)S(1)} all-to-all(f32[4,256,256]{2,1,0:T(8,128)S(1)} %broadcast_in_dim.16), channel_id=1, replica_groups=mesh['row'=4,'col'=32] {'row'}, dimensions={0} | all-to-all | bytes 2097152 | tf_op jit(solution)/shard_map/all_to_all | solution.py:22
  87.0 12.5 %convolution_subtract_fusion.7 = f32[4096,256]{1,0:T(8,128)} fusion(f32[4096,256]{1,0:T(8,128)} %param.3, f32[256,256]{1,0:T(8,128)S(1)} %fusion.38, f32[256,4352]{1,0:T(8,128)} %all-gather.9.cloned.1.call-done), kind=kOutput, calls=%fused_computation.7 | convolution fusion | flops 3222274048 | bytes 12845056 | tf_op jit(solution)/shard_map/dot_general | solution.py:30
  99.6 6.6 %all-gather.11.cloned.1.call-done = f32[256,4352]{1,0:T(8,128)} async-done(((f32[8,4352]{1,0:T(8,128)}), f32[256,4352]{1,0:T(8,128)}) %all-gather.11.cloned.1.call-update) | async-done | bytes 4456464 | tf_op jit(solution)/shard_map/all_gather | solution.py:12
  106.1 7.0 %fusion.19 = f32[256,256]{1,0:T(8,128)S(1)} fusion(f32[4096,256]{1,0:T(8,128)} %convolution_subtract_fusion.7, f32[256,4352]{1,0:T(8,128)} %all-gather.11.cloned.1.call-done), kind=kOutput, calls=%fused_computation.27 | convolution fusion | flops 3221225472 | bytes 8650752 | tf_op jit(solution)/shard_map/dot_general | solution.py:34
  113.3 20.2 %all_to_all.41 = f32[4,256,256]{2,1,0:T(8,128)S(1)} all-to-all(f32[4,256,256]{2,1,0:T(8,128)S(1)} %broadcast_in_dim.17), channel_id=1, replica_groups=mesh['row'=4,'col'=32] {'row'}, dimensions={0} | all-to-all | bytes 2097152 | tf_op jit(solution)/shard_map/all_to_all | solution.py:22
  135.1 12.5 %convolution_subtract_fusion.6 = f32[4096,256]{1,0:T(8,128)} fusion(f32[4096,256]{1,0:T(8,128)} %convolution_subtract_fusion.7, f32[256,256]{1,0:T(8,128)S(1)} %fusion.36, f32[256,4352]{1,0:T(8,128)} %all-gather.11.cloned.1.call-done), kind=kOutput, calls=%fused_computation.6 | convolution fusion | flops 3222274048 | bytes 12845056 | tf_op jit(solution)/shard_map/dot_general | solution.py:30
  147.7 6.3 %all-gather.13.cloned.1.call-done = f32[256,4352]{1,0:T(8,128)} async-done(((f32[8,4352]{1,0:T(8,128)}), f32[256,4352]{1,0:T(8,128)}) %all-gather.13.cloned.1.call-update) | async-done | bytes 4456464 | tf_op jit(solution)/shard_map/all_gather | solution.py:12
  154.0 7.0 %fusion.16 = f32[256,256]{1,0:T(8,128)S(1)} fusion(f32[4096,256]{1,0:T(8,128)} %convolution_subtract_fusion.6, f32[256,4352]{1,0:T(8,128)} %all-gather.13.cloned.1.call-done), kind=kOutput, calls=%fused_computation.24 | convolution fusion | flops 3221225472 | bytes 8650752 | tf_op jit(solution)/shard_map/dot_general | solution.py:34
  167.4 14.6 %all-to-all-done.2 = f32[4,256,256]{2,1,0:T(8,128)S(1)} async-done(((f32[4,256,256]{2,1,0:T(8,128)}), f32[4,256,256]{2,1,0:T(8,128)S(1)}, u32[]{:S(2)}, u32[]{:S(2)}) %all-to-all-start.2) | async-done | bytes 1048608 | tf_op jit(solution)/shard_map/all_to_all | solution.py:22
  183.7 12.5 %convolution_subtract_fusion.5 = f32[4096,256]{1,0:T(8,128)} fusion(f32[4096,256]{1,0:T(8,128)} %convolution_subtract_fusion.6, f32[256,256]{1,0:T(8,128)S(1)} %fusion.34, f32[256,4352]{1,0:T(8,128)} %all-gather.13.cloned.1.call-done), kind=kOutput, calls=%fused_computation.5 | convolution fusion | flops 3222274048 | bytes 12845056 | tf_op jit(solution)/shard_map/dot_general | solution.py:30
  196.2 5.5 %all-gather.15.cloned.1.call-done = f32[256,4352]{1,0:T(8,128)} async-done(((f32[8,4352]{1,0:T(8,128)}), f32[256,4352]{1,0:T(8,128)}) %all-gather.15.cloned.1.call-update) | async-done | bytes 4456464 | tf_op jit(solution)/shard_map/all_gather | solution.py:12
  201.8 7.0 %fusion.13 = f32[256,256]{1,0:T(8,128)S(1)} fusion(f32[4096,256]{1,0:T(8,128)} %convolution_subtract_fusion.5, f32[256,4352]{1,0:T(8,128)} %all-gather.15.cloned.1.call-done), kind=kOutput, calls=%fused_computation.21 | convolution fusion | flops 3221225472 | bytes 8650752 | tf_op jit(solution)/shard_map/dot_general | solution.py:34
  208.9 19.9 %all_to_all.42 = f32[4,256,256]{2,1,0:T(8,128)S(1)} all-to-all(f32[4,256,256]{2,1,0:T(8,128)S(1)} %broadcast_in_dim.19), channel_id=1, replica_groups=mesh['row'=4,'col'=32] {'row'}, dimensions={0} | all-to-all | bytes 2097152 | tf_op jit(solution)/shard_map/all_to_all | solution.py:22
  230.4 12.5 %convolution_subtract_fusion.4 = f32[4096,256]{1,0:T(8,128)} fusion(f32[4096,256]{1,0:T(8,128)} %convolution_subtract_fusion.5, f32[256,256]{1,0:T(8,128)S(1)} %fusion.32, f32[256,4352]{1,0:T(8,128)} %all-gather.15.cloned.1.call-done), kind=kOutput, calls=%fused_computation.4 | convolution fusion | flops 3222274048 | bytes 12845056 | tf_op jit(solution)/shard_map/dot_general | solution.py:30
  243.0 6.5 %all-gather.17.cloned.1.call-done = f32[256,4352]{1,0:T(8,128)} async-done(((f32[8,4352]{1,0:T(8,128)}), f32[256,4352]{1,0:T(8,128)}) %all-gather.17.cloned.1.call-update) | async-done | bytes 4456464 | tf_op jit(solution)/shard_map/all_gather | solution.py:12
  249.5 7.0 %fusion.10 = f32[256,256]{1,0:T(8,128)S(1)} fusion(f32[4096,256]{1,0:T(8,128)} %convolution_subtract_fusion.4, f32[256,4352]{1,0:T(8,128)} %all-gather.17.cloned.1.call-done), kind=kOutput, calls=%fused_computation.18 | convolution fusion | flops 3221225472 | bytes 8650752 | tf_op jit(solution)/shard_map/dot_general | solution.py:34
  256.6 20.1 %all_to_all.43 = f32[4,256,256]{2,1,0:T(8,128)S(1)} all-to-all(f32[4,256,256]{2,1,0:T(8,128)S(1)} %broadcast_in_dim.20), channel_id=1, replica_groups=mesh['row'=4,'col'=32] {'row'}, dimensions={0} | all-to-all | bytes 2097152 | tf_op jit(solution)/shard_map/all_to_all | solution.py:22
  278.4 12.5 %convolution_subtract_fusion.3 = f32[4096,256]{1,0:T(8,128)} fusion(f32[4096,256]{1,0:T(8,128)} %convolution_subtract_fusion.4, f32[256,256]{1,0:T(8,128)S(1)} %fusion.30, f32[256,4352]{1,0:T(8,128)} %all-gather.17.cloned.1.call-done), kind=kOutput, calls=%fused_computation.3 | convolution fusion | flops 3222274048 | bytes 12845056 | tf_op jit(solution)/shard_map/dot_general | solution.py:30
  290.9 6.3 %all-gather.19.cloned.1.call-done = f32[256,4352]{1,0:T(8,128)} async-done(((f32[8,4352]{1,0:T(8,128)}), f32[256,4352]{1,0:T(8,128)}) %all-gather.19.cloned.1.call-update) | async-done | bytes 4456464 | tf_op jit(solution)/shard_map/all_gather | solution.py:12
  297.2 7.0 %fusion.7 = f32[256,256]{1,0:T(8,128)S(1)} fusion(f32[4096,256]{1,0:T(8,128)} %convolution_subtract_fusion.3, f32[256,4352]{1,0:T(8,128)} %all-gather.19.cloned.1.call-done), kind=kOutput, calls=%fused_computation.15 | convolution fusion | flops 3221225472 | bytes 8650752 | tf_op jit(solution)/shard_map/dot_general | solution.py:34
  304.4 19.9 %all_to_all.44 = f32[4,256,256]{2,1,0:T(8,128)S(1)} all-to-all(f32[4,256,256]{2,1,0:T(8,128)S(1)} %broadcast_in_dim.21), channel_id=1, replica_groups=mesh['row'=4,'col'=32] {'row'}, dimensions={0} | all-to-all | bytes 2097152 | tf_op jit(solution)/shard_map/all_to_all | solution.py:22
  325.9 12.4 %convolution_subtract_fusion.2 = f32[4096,256]{1,0:T(8,128)} fusion(f32[4096,256]{1,0:T(8,128)} %convolution_subtract_fusion.3, f32[256,256]{1,0:T(8,128)S(1)} %fusion.28, f32[256,4352]{1,0:T(8,128)} %all-gather.19.cloned.1.call-done), kind=kOutput, calls=%fused_computation.2 | convolution fusion | flops 3222274048 | bytes 12845056 | tf_op jit(solution)/shard_map/dot_general | solution.py:30
  338.3 6.8 %all-gather.21.cloned.1.call-done = f32[256,4352]{1,0:T(8,128)} async-done(((f32[8,4352]{1,0:T(8,128)}), f32[256,4352]{1,0:T(8,128)}) %all-gather.21.cloned.1.call-update) | async-done | bytes 4456464 | tf_op jit(solution)/shard_map/all_gather | solution.py:12
  345.1 7.0 %fusion.4 = f32[256,256]{1,0:T(8,128)S(1)} fusion(f32[4096,256]{1,0:T(8,128)} %convolution_subtract_fusion.2, f32[256,4352]{1,0:T(8,128)} %all-gather.21.cloned.1.call-done), kind=kOutput, calls=%fused_computation.12 | convolution fusion | flops 3221225472 | bytes 8650752 | tf_op jit(solution)/shard_map/dot_general | solution.py:34
  352.2 19.9 %all_to_all.45 = f32[4,256,256]{2,1,0:T(8,128)S(1)} all-to-all(f32[4,256,256]{2,1,0:T(8,128)S(1)} %broadcast_in_dim.22), channel_id=1, replica_groups=mesh['row'=4,'col'=32] {'row'}, dimensions={0} | all-to-all | bytes 2097152 | tf_op jit(solution)/shard_map/all_to_all | solution.py:22
  373.8 12.5 %convolution_subtract_fusion.1 = f32[4096,256]{1,0:T(8,128)} fusion(f32[4096,256]{1,0:T(8,128)} %convolution_subtract_fusion.2, f32[256,256]{1,0:T(8,128)S(1)} %fusion.26, f32[256,4352]{1,0:T(8,128)} %all-gather.21.cloned.1.call-done), kind=kOutput, calls=%fused_computation.1 | convolution fusion | flops 3222274048 | bytes 12845056 | tf_op jit(solution)/shard_map/dot_general | solution.py:30
  386.3 6.7 %all-gather.23.cloned.1.call-done = f32[256,4352]{1,0:T(8,128)} async-done(((f32[8,4352]{1,0:T(8,128)}), f32[256,4352]{1,0:T(8,128)}) %all-gather.23.cloned.1.call-update) | async-done | bytes 4456464 | tf_op jit(solution)/shard_map/all_gather | solution.py:12
  393.0 7.0 %fusion.1 = f32[256,256]{1,0:T(8,128)S(1)} fusion(f32[4096,256]{1,0:T(8,128)} %convolution_subtract_fusion.1, f32[256,4352]{1,0:T(8,128)} %all-gather.23.cloned.1.call-done), kind=kOutput, calls=%fused_computation.9 | convolution fusion | flops 3221225472 | bytes 8650752 | tf_op jit(solution)/shard_map/dot_general | solution.py:34
  400.1 20.0 %all_to_all.46 = f32[4,256,256]{2,1,0:T(8,128)S(1)} all-to-all(f32[4,256,256]{2,1,0:T(8,128)S(1)} %broadcast_in_dim.23), channel_id=1, replica_groups=mesh['row'=4,'col'=32] {'row'}, dimensions={0} | all-to-all | bytes 2097152 | tf_op jit(solution)/shard_map/all_to_all | solution.py:22
  421.7 12.2 %convolution_subtract_fusion = f32[4096,256]{1,0:T(8,128)} fusion(f32[4096,256]{1,0:T(8,128)} %convolution_subtract_fusion.1, f32[256,256]{1,0:T(8,128)S(1)} %fusion.24, f32[256,4352]{1,0:T(8,128)} %all-gather.23.cloned.1.call-done), kind=kOutput, calls=%fused_computation | convolution fusion | flops 3222274048 | bytes 12845056 | tf_op jit(solution)/shard_map/dot_general | solution.py:30
  (51 shorter events, 27.1 us)
Async XLA Ops:
  6.5 51.7 %all-gather.9.cloned.1.call-start = ((), (), s32[]{:S(2)}) async-start(), calls=%async_computation.8 | async-start | bytes 4595712 | tf_op jit(solution)/shard_map/all_gather | solution.py:12
  9.4 96.7 %all-gather.11.cloned.1.call-start = ((), (), s32[]{:S(2)}) async-start(), calls=%async_computation.9 | async-start | bytes 4595712 | tf_op jit(solution)/shard_map/all_gather | solution.py:12
  10.2 143.9 %all-gather.13.cloned.1.call-start = ((), (), s32[]{:S(2)}) async-start(), calls=%async_computation.10 | async-start | bytes 4595712 | tf_op jit(solution)/shard_map/all_gather | solution.py:12
  10.9 190.8 %all-gather.15.cloned.1.call-start = ((), (), s32[]{:S(2)}) async-start(), calls=%async_computation.11 | async-start | bytes 4595712 | tf_op jit(solution)/shard_map/all_gather | solution.py:12
  11.7 237.8 %all-gather.17.cloned.1.call-start = ((), (), s32[]{:S(2)}) async-start(), calls=%async_computation.12 | async-start | bytes 4595712 | tf_op jit(solution)/shard_map/all_gather | solution.py:12
  12.4 284.8 %all-gather.19.cloned.1.call-start = ((), (), s32[]{:S(2)}) async-start(), calls=%async_computation.13 | async-start | bytes 4595712 | tf_op jit(solution)/shard_map/all_gather | solution.py:12
  13.2 331.9 %all-gather.21.cloned.1.call-start = ((), (), s32[]{:S(2)}) async-start(), calls=%async_computation.14 | async-start | bytes 4595712 | tf_op jit(solution)/shard_map/all_gather | solution.py:12
  162.2 19.9 %all-to-all-start.2 = ((f32[4,256,256]{2,1,0:T(8,128)}), f32[4,256,256]{2,1,0:T(8,128)S(1)}, u32[]{:S(2)}, u32[]{:S(2)}) async-start(f32[4,256,256]{2,1,0:T(8,128)} %broadcast_in_dim.18), calls=%async_computation.2 | async-start | bytes 2097152 | tf_op jit(solution)/shard_map/all_to_all | solution.py:22
  166.6 226.4 %all-gather.23.cloned.1.call-start = ((), (), s32[]{:S(2)}) async-start(), calls=%async_computation.15 | async-start | bytes 4595712 | tf_op jit(solution)/shard_map/all_gather | solution.py:12
Sparse Core Ops, SparseCore 0:
  9.6 48.6 all-gather.8
  60.5 45.5 all-gather.10
  108.4 45.5 all-gather.12
  156.1 45.5 all-gather.14
  203.9 45.5 all-gather.16
  251.6 45.5 all-gather.18
  299.5 45.5 all-gather.20
  347.3 45.5 all-gather.22
where the time goes:
time: 444 us; the launch traced here: 441 us
  matrix products  169 us (38%)
  blocking collectives  140 us (32%)
  waiting for transfers between devices  104 us (23%)
  between operations  14 us (3%)
  other arithmetic  5.98 us (1%)
  starting transfers between devices  4.84 us (1%)
    all_to_all x7, blocking collectives, copy_for_each(): lax.all_to_all(jnp.broadcast_to(x[None], (length, *x.shape)), axis, 0, 0,...  140 us
    dot_general x16, matrix products, matmul(): jnp.dot(left, right, preferred_element_type=jnp.float32, precision=exact_...  112 us
    all_gather x8, waiting for transfers between devices, gather_turned(): result, at, done = (lax.all_gather(both, axis, axis=0, tiled=True), 0, [])  89.1 us
    dot_general x8, matrix products, project(): lax.dot_general(left, right, (((0,), (0,)), ((), ())), precision=exact_pr...  56.4 us
    all_to_all x1, waiting for transfers between devices, copy_for_each(): lax.all_to_all(jnp.broadcast_to(x[None], (length, *x.shape)), axis, 0, 0,...  14.6 us
  transfers between devices with their start and end apart: 9, of which 9 were waited for; matrix products, arithmetic and copies ran while one was open for 35% of the time, Pallas kernels for 0%

commit v1 on v0

v1 whole, which is shorter than its diff:
```python
import jax
import jax.numpy as jnp
from jax import lax
from jax.experimental import pallas as pl
from jax.experimental.pallas import tpu as pltpu
from jax.sharding import PartitionSpec as P

MESH = pl.DeviceIdType.MESH
F32, BF16 = jnp.float32, jnp.bfloat16
PANELS, WIDTH, ROWS, COLS = 8, 256, 4096, 256
SIDE, STRIPE = 4, 8
LANES = ROWS + WIDTH
CHUNK = 1024
SPANS = ((0, 1024), (1024, 1024), (2048, 1024), (3072, 1280))
QUARTERS = len(SPANS)
BLOCK = 512
AHEAD = 2


def halves(x):
    high = x.astype(BF16)
    return high, (x - high.astype(F32)).astype(BF16)


def dot3(left, right):
    (lh, ll), (rh, rl) = left, right
    dot = lambda u, v: jnp.dot(u, v, preferred_element_type=F32)
    return dot(lh, rh) + dot(lh, rl) + dot(ll, rh)


def kernel(
    z_in, v_in, t_in, z_out,
    vbuf, z, zh, zl, vh, vl, vnh, vnl, proj, gram, psend, prec, sfull, sh, sl,
    load_sem, z_sem, out_sem,
    near_sem, half_sem, row_sem, rowhalf_sem, core_sem, sent1, sent2, sent3,
    rs_sem, rs_sent, ag_sem, ag_sent,
):
    row, col = lax.axis_index("row"), lax.axis_index("col")
    core, x, y = lax.rem(col, 2), lax.rem(col // 2, SIDE), col // (2 * SIDE)
    a, b = x + core * (y - x), y + core * (x - y)
    step_a, step_b = 1 + 3 * core, 4 - 3 * core
    wrap = lambda i: lax.rem(i + SIDE, SIDE)

    def at(a_to, b_to):
        return (row, 2 * (a_to * step_a + b_to * step_b) + core)

    a_next, a_prev, b_next, b_prev = wrap(a + 1), wrap(a - 1), wrap(b + 1), wrap(b - 1)
    a_far, b_far = wrap(a + 2), wrap(b + 2)
    up_a, down_a, up_b, down_b = at(a_next, b), at(a_prev, b), at(a, b_next), at(a, b_prev)
    partner = (row, col + 1 - 2 * core)
    lifts = [(wrap(row + d), col) for d in (1, 2, 3)]

    def copy(src, dst, send, recv, device):
        return pltpu.make_async_remote_copy(
            src_ref=src, dst_ref=dst, send_sem=send, recv_sem=recv, device_id=device, device_id_type=MESH
        )

    def push(ref, send, recv, device):
        copy(ref, ref, send, recv, device).start()

    def arrived(ref, recv):
        copy(ref, ref, sent1.at[0], recv, partner).wait_recv()

    def gone(ref, send):
        copy(ref, ref, send, core_sem.at[0, 0], partner).wait_send()

    def stripe(n, q, a_of, part=None):
        start, size = SPANS[q]
        if part is not None:
            size //= 2
            start += part * size
        return vbuf.at[n, core, b, a_of, :, pl.ds(start, size)]

    def line(n, q, b_of, part=None):
        start, size = SPANS[q]
        first, count = (0, SIDE) if part is None else (2 * part, 2)
        return vbuf.at[n, core, b_of, pl.ds(first, count), :, pl.ds(start, size)]

    def load(n):
        own = lambda start, size: vbuf.at[n, core, b, a, :, pl.ds(start, size)]
        return (
            pltpu.make_async_copy(v_in.at[PANELS - 1 - n], own(0, ROWS), load_sem.at[n, 0]),
            pltpu.make_async_copy(t_in.at[PANELS - 1 - n], own(ROWS, WIDTH), load_sem.at[n, 1]),
        )

    def wait_load(n):
        for one in load(n):
            one.wait()

    def first_send(n, q):
        push(stripe(n, q, a), sent1.at[n], near_sem.at[n, q, 0], up_a)
        push(stripe(n, q, a), sent1.at[n], near_sem.at[n, q, 1], down_a)

    def stage_a(n, q):
        arrived(stripe(n, q, a_prev), near_sem.at[n, q, 0])
        push(stripe(n, q, a_prev, 0), sent1.at[n], half_sem.at[n, q, 0], up_a)
        arrived(stripe(n, q, a_next), near_sem.at[n, q, 1])
        push(stripe(n, q, a_next, 1), sent1.at[n], half_sem.at[n, q, 1], down_a)

    def stage_b(n, q):
        arrived(stripe(n, q, a_far, 0), half_sem.at[n, q, 0])
        arrived(stripe(n, q, a_far, 1), half_sem.at[n, q, 1])
        push(line(n, q, b), sent2.at[n], row_sem.at[n, q, 0], up_b)
        push(line(n, q, b), sent2.at[n], row_sem.at[n, q, 1], down_b)
        push(line(n, q, b), sent3.at[n], core_sem.at[n, q], partner)

    def stage_c(n, q):
        arrived(line(n, q, b_prev), row_sem.at[n, q, 0])
        push(line(n, q, b_prev, 0), sent2.at[n], rowhalf_sem.at[n, q, 0], up_b)
        push(line(n, q, b_prev), sent3.at[n], core_sem.at[n, q], partner)
        arrived(line(n, q, b_next), row_sem.at[n, q, 1])
        push(line(n, q, b_next, 1), sent2.at[n], rowhalf_sem.at[n, q, 1], down_b)
        push(line(n, q, b_next), sent3.at[n], core_sem.at[n, q], partner)

    def stage_d(n, q):
        arrived(line(n, q, b_far, 0), rowhalf_sem.at[n, q, 0])
        arrived(line(n, q, b_far, 1), rowhalf_sem.at[n, q, 1])
        push(line(n, q, b_far), sent3.at[n], core_sem.at[n, q], partner)

    def stage_e(n, q):
        start, size = SPANS[q]
        arrived(vbuf.at[n, 1 - core, :, :, :, pl.ds(start, size)], core_sem.at[n, q])

    def pair(n, i, start, size):
        yy, xx = divmod(i, SIDE)
        lanes = pl.ds(start, size)
        return jnp.concatenate([vbuf[n, 0, yy, xx, :, lanes], vbuf[n, 1, xx, yy, :, lanes]], axis=0)

    def absorb(n, q):
        slot = lax.rem(n, 2)
        rows = pl.ds(CHUNK * q, CHUNK)
        for i in range(SIDE * SIDE):
            high, low = halves(pair(n, i, CHUNK * q, CHUNK))
            vh[pl.ds(2 * STRIPE * i, 2 * STRIPE), :] = high
            vl[pl.ds(2 * STRIPE * i, 2 * STRIPE), :] = low
        vnh[slot, rows, :] = vh[...].T
        vnl[slot, rows, :] = vl[...].T
        left = (vh[...], vl[...])
        part = dot3(left, (zh[rows, :], zl[rows, :]))
        proj[...] = part if q == 0 else proj[...] + part

        @pl.when(n > 0)
        def _():
            part = dot3(left, (vnh[1 - slot, rows, :], vnl[1 - slot, rows, :]))
            gram[...] = part if q == 0 else gram[...] + part

    quarter = COLS // 4
    own_rows = pl.ds(pl.multiple_of(quarter * row, quarter), quarter)

    def take_s(n):
        for d in (1, 2, 3):
            rows = pl.ds(pl.multiple_of(quarter * wrap(row - d), quarter), quarter)
            arrived(sfull.at[n, rows], ag_sem.at[n, d - 1])
        sh[...], sl[...] = halves(sfull[n].T)

    def finish(n):
        @pl.when(n > 0)
        def _():
            take_s(n - 1)
            proj[...] = proj[...] - dot3(halves(gram[...]), (sh[...], sl[...]))

        psend[n] = proj[...].T
        for d in (1, 2, 3):
            rows = pl.ds(pl.multiple_of(quarter * wrap(row + d), quarter), quarter)
            copy(psend.at[n, rows], prec.at[n, d - 1], rs_sent.at[n], rs_sem.at[n, d - 1], lifts[d - 1]).start()

    def scale(n):
        total = psend[n, own_rows, :]
        for d in (1, 2, 3):
            arrived(prec.at[n, d - 1], rs_sem.at[n, d - 1])
        for d in (1, 2, 3):
            total = total + prec[n, d - 1]
        factor = jnp.concatenate([pair(n, i, ROWS, WIDTH) for i in range(SIDE * SIDE)], axis=0)
        sfull[n, own_rows, :] = dot3(halves(total), halves(factor))
        for d in (1, 2, 3):
            push(sfull.at[n, own_rows], ag_sent.at[n], ag_sem.at[n, d - 1], lifts[d - 1])

    def write(i):
        rows = pl.ds(pl.multiple_of(i * BLOCK, BLOCK), BLOCK)
        return pltpu.make_async_copy(z.at[rows], z_out.at[rows], out_sem.at[i])

    def update(n, last=False):
        slot = lax.rem(n, 2)

        def body(i, carry):
            rows = pl.ds(pl.multiple_of(i * BLOCK, BLOCK), BLOCK)
            new = z[rows, :] - dot3((vnh[slot, rows, :], vnl[slot, rows, :]), (sh[...], sl[...]))
            z[rows, :] = new
            if last:
                write(i).start()
            else:
                zh[rows, :], zl[rows, :] = halves(new)
            return carry

        lax.fori_loop(0, ROWS // BLOCK, body, 0)

    z_load = pltpu.make_async_copy(z_in, z, z_sem)

    def start_load(n, carry):
        for one in load(n):
            one.start()
        return carry

    lax.fori_loop(0, PANELS, start_load, 0)
    z_load.start()

    barrier = pltpu.get_barrier_semaphore()
    greeted = [up_a, down_a, up_b, down_b, partner] + lifts
    for device in greeted:
        pl.semaphore_signal(barrier, inc=1, device_id=device, device_id_type=MESH)
    pl.semaphore_wait(barrier, len(greeted))

    def open_sends(n, carry):
        wait_load(n)
        for q in range(QUARTERS):
            first_send(n, q)
        return carry

    lax.fori_loop(0, AHEAD, open_sends, 0)
    z_load.wait()

    def split_z(i, carry):
        rows = pl.ds(pl.multiple_of(i * BLOCK, BLOCK), BLOCK)
        zh[rows, :], zl[rows, :] = halves(z[rows, :])
        return carry

    lax.fori_loop(0, ROWS // BLOCK, split_z, 0)

    def panel(p, carry):
        for q in range(QUARTERS):

            @pl.when(p + AHEAD < PANELS)
            def _():
                if q == 0:
                    wait_load(p + AHEAD)
                first_send(p + AHEAD, q)

            for back, stage in ((0, stage_a), (1, stage_b), (2, stage_c), (3, stage_d)):
                behind, at_q = (0, q - back) if q >= back else (1, q - back + QUARTERS)
                when = (p < PANELS) if behind == 0 else (p > 0)
                pl.when(when)(lambda: stage(p - behind, at_q))

            n = p - 1

            @pl.when(p > 0)
            def _():
                stage_e(n, q)
                if q == 0:
                    pl.when(n > 1)(lambda: update(n - 2))
                absorb(n, q)
                if q == 1:
                    pl.when(n > 0)(lambda: scale(n - 1))
                if q == QUARTERS - 1:
                    finish(n)

        return carry

    lax.fori_loop(0, PANELS + 1, panel, 0)

    update(PANELS - 2)
    scale(PANELS - 1)
    take_s(PANELS - 1)
    update(PANELS - 1, last=True)

    def close(n, carry):
        gone(vbuf.at[n, 0, 0, pl.ds(0, 3)], sent1.at[n])
        gone(vbuf.at[n, 0, pl.ds(0, 3)], sent2.at[n])
        gone(vbuf.at[n, 0], sent3.at[n])
        gone(prec.at[n], rs_sent.at[n])
        gone(prec.at[n], ag_sent.at[n])
        return carry

    lax.fori_loop(0, PANELS, close, 0)

    def close_out(i, carry):
        write(i).wait()
        return carry

    lax.fori_loop(0, ROWS // BLOCK, close_out, 0)


def local(eigvecs, v_panels, t_panels):
    dma = pltpu.SemaphoreType.DMA
    anywhere = pl.BlockSpec(memory_space=pl.ANY)
    return pl.pallas_call(
        kernel,
        out_shape=jax.ShapeDtypeStruct((ROWS, COLS), F32),
        in_specs=[anywhere] * 3,
        out_specs=anywhere,
        scratch_shapes=[
            pltpu.VMEM((PANELS, 2, SIDE, SIDE, STRIPE, LANES), F32),
            pltpu.VMEM((ROWS, COLS), F32),
            pltpu.VMEM((ROWS, COLS), BF16),
            pltpu.VMEM((ROWS, COLS), BF16),
            pltpu.VMEM((WIDTH, CHUNK), BF16),
            pltpu.VMEM((WIDTH, CHUNK), BF16),
            pltpu.VMEM((2, ROWS, WIDTH), BF16),
            pltpu.VMEM((2, ROWS, WIDTH), BF16),
            pltpu.VMEM((WIDTH, COLS), F32),
            pltpu.VMEM((WIDTH, WIDTH), F32),
            pltpu.VMEM((PANELS, COLS, WIDTH), F32),
            pltpu.VMEM((PANELS, 3, COLS // 4, WIDTH), F32),
            pltpu.VMEM((PANELS, COLS, WIDTH), F32),
            pltpu.VMEM((WIDTH, COLS), BF16),
            pltpu.VMEM((WIDTH, COLS), BF16),
            dma((PANELS, 2)),
            dma,
            dma((ROWS // BLOCK,)),
            dma((PANELS, QUARTERS, 2)),
            dma((PANELS, QUARTERS, 2)),
            dma((PANELS, QUARTERS, 2)),
            dma((PANELS, QUARTERS, 2)),
            dma((PANELS, QUARTERS)),
            dma((PANELS,)),
            dma((PANELS,)),
            dma((PANELS,)),
            dma((PANELS, 3)),
            dma((PANELS,)),
            dma((PANELS, 3)),
            dma((PANELS,)),
        ],
        compiler_params=pltpu.CompilerParams(
            collective_id=0, has_side_effects=True, vmem_limit_bytes=67043328
        ),
    )(eigvecs, jnp.swapaxes(v_panels, 1, 2), jnp.swapaxes(t_panels, 1, 2))


def solution(mesh):
    in_specs = (P("row", "col"), P(None, "row", "col"), P(None, None, "col"))
    out_specs = P("row", "col")
    return jax.shard_map(local, mesh=mesh, in_specs=in_specs, out_specs=out_specs, check_vma=False)
```

time: 444 us -> 171 us (0.39)
  matrix products: 169 us -> 0 us
  Pallas kernels: 0 us -> 167 us
  blocking collectives: 140 us -> 0 us
  waiting for transfers between devices: 104 us -> 0 us
  between operations: 14 us -> 0.01 us
  other arithmetic: 5.98 us -> 0 us
  starting transfers between devices: 4.84 us -> 0 us
    dot_general x24 -> x0, matrix products: 169 us -> none  [the longest x16 112 us: matmul(): jnp.dot(left, right, preferred_element_type=jnp.float32, precision=exact_...]
    pallas_call x0 -> x1, Pallas kernels: none -> 167 us  [local(): pl.pallas_call(kernel, out_shape=jax.ShapeDtypeStruct((ROWS, COLS), F32),...]
    all_to_all x7 -> x0, blocking collectives: 140 us -> none  [copy_for_each(): lax.all_to_all(jnp.broadcast_to(x[None], (length, *x.shape)), axis, 0, 0,...]
    all_gather x8 -> x0, waiting for transfers between devices: 89.1 us -> none  [gather_turned(): result, at, done = (lax.all_gather(both, axis, axis=0, tiled=True), 0, [])]
    all_to_all x1 -> x0, waiting for transfers between devices: 14.6 us -> none  [copy_for_each(): lax.all_to_all(jnp.broadcast_to(x[None], (length, *x.shape)), axis, 0, 0,...]
    concatenate x8 -> x0, other arithmetic: 5.36 us -> none  [gather_turned(): both = jnp.concatenate([t.reshape(len(t), -1) for t in turned], axis=1)]
    unnamed x0 -> x1, local copies, waits for them, and re-layouts: none -> 4.47 us
  transfers between devices with their start and end apart: 9 -> 0, of which waited for: 9 -> 0; matrix products, arithmetic and copies ran while one was open for 35% -> 0% of each run, Pallas kernels for 0% -> 0%
where the time goes in v1:
time: 171 us
  Pallas kernels  167 us (98%)
  local copies, waits for them, and re-layouts  4.47 us (3%)
    pallas_call x1, Pallas kernels, local(): pl.pallas_call(kernel, out_shape=jax.ShapeDtypeStruct((ROWS, COLS), F32),...  167 us
    unnamed x1, local copies, waits for them, and re-layouts  4.47 us

profile of v1, /device:TPU:0, one launch (start us, length us, event | category | flops | bytes accessed | tf_op | source)
XLA Modules:
  0.0 171.2 jit_solution(15445858563029080815)
XLA Ops:
  0.0 166.7 %shard_map.37 = f32[4096,256]{1,0:T(8,128)} custom-call(f32[4096,256]{1,0:T(8,128)} %z_in.1, f32[8,8,4096]{2,1,0:T(8,128)} %bitcast.2, f32[8,8,256]{2,1,0:T(8,128)} %bitcast.3), custom_call_target="tpu_custom_call" | custom-call | tf_op jit(solution)/shard_map/pallas_call | solution.py:285
  166.7 4.5 %copy.5 = f32[4096,256]{1,0:T(8,128)} copy(f32[4096,256]{1,0:T(8,128)} %shard_map.37) | data formatting | bytes 8388608

commit v2 on v1

--- a/solution.py
+++ b/solution.py
@@ -15,6 +15,7 @@
 QUARTERS = len(SPANS)
 BLOCK = 512
 AHEAD = 2
+LAGS = (0, 2, 4, 6, 8)
 
 
 def halves(x):
@@ -29,9 +30,9 @@
 
 
 def kernel(
-    z_in, v_in, t_in, z_out,
-    vbuf, z, zh, zl, vh, vl, vnh, vnl, proj, gram, psend, prec, sfull, sh, sl,
-    load_sem, z_sem, out_sem,
+    z_in, v_in, t_in, z,
+    vbuf, zh, zl, vh, vl, vnh, vnl, both, psend, prec, sfull, sh, sl,
+    load_sem, z_sem,
     near_sem, half_sem, row_sem, rowhalf_sem, core_sem, sent1, sent2, sent3,
     rs_sem, rs_sent, ag_sem, ag_sent,
 ):
@@ -135,14 +136,12 @@
             vl[pl.ds(2 * STRIPE * i, 2 * STRIPE), :] = low
         vnh[slot, rows, :] = vh[...].T
         vnl[slot, rows, :] = vl[...].T
-        left = (vh[...], vl[...])
-        part = dot3(left, (zh[rows, :], zl[rows, :]))
-        proj[...] = part if q == 0 else proj[...] + part
-
-        @pl.when(n > 0)
-        def _():
-            part = dot3(left, (vnh[1 - slot, rows, :], vnl[1 - slot, rows, :]))
-            gram[...] = part if q == 0 else gram[...] + part
+        right = (
+            jnp.concatenate([zh[rows, :], vnh[1 - slot, rows, :]], axis=1),
+            jnp.concatenate([zl[rows, :], vnl[1 - slot, rows, :]], axis=1),
+        )
+        part = dot3((vh[...], vl[...]), right)
+        both[...] = part if q == 0 else both[...] + part
 
     quarter = COLS // 4
     own_rows = pl.ds(pl.multiple_of(quarter * row, quarter), quarter)
@@ -154,12 +153,15 @@
         sh[...], sl[...] = halves(sfull[n].T)
 
     def finish(n):
+        @pl.when(n == 0)
+        def _():
+            psend[n] = both[:, :COLS].T
+
         @pl.when(n > 0)
         def _():
             take_s(n - 1)
-            proj[...] = proj[...] - dot3(halves(gram[...]), (sh[...], sl[...]))
-
-        psend[n] = proj[...].T
+            psend[n] = (both[:, :COLS] - dot3(halves(both[:, COLS:]), (sh[...], sl[...]))).T
+
         for d in (1, 2, 3):
             rows = pl.ds(pl.multiple_of(quarter * wrap(row + d), quarter), quarter)
             copy(psend.at[n, rows], prec.at[n, d - 1], rs_sent.at[n], rs_sem.at[n, d - 1], lifts[d - 1]).start()
@@ -175,9 +177,11 @@
         for d in (1, 2, 3):
             push(sfull.at[n, own_rows], ag_sent.at[n], ag_sem.at[n, d - 1], lifts[d - 1])
 
-    def write(i):
-        rows = pl.ds(pl.multiple_of(i * BLOCK, BLOCK), BLOCK)
-        return pltpu.make_async_copy(z.at[rows], z_out.at[rows], out_sem.at[i])
+    def update_rows(n, q):
+        slot, rows = lax.rem(n, 2), pl.ds(CHUNK * q, CHUNK)
+        new = z[rows, :] - dot3((vnh[slot, rows, :], vnl[slot, rows, :]), (sh[...], sl[...]))
+        z[rows, :] = new
+        zh[rows, :], zl[rows, :] = halves(new)
 
     def update(n, last=False):
         slot = lax.rem(n, 2)
@@ -186,9 +190,7 @@
             rows = pl.ds(pl.multiple_of(i * BLOCK, BLOCK), BLOCK)
             new = z[rows, :] - dot3((vnh[slot, rows, :], vnl[slot, rows, :]), (sh[...], sl[...]))
             z[rows, :] = new
-            if last:
-                write(i).start()
-            else:
+            if not last:
                 zh[rows, :], zl[rows, :] = halves(new)
             return carry
 
@@ -227,6 +229,9 @@
     lax.fori_loop(0, ROWS // BLOCK, split_z, 0)
 
     def panel(p, carry):
+        def behind(q, lag):
+            return p + (q - lag) // QUARTERS, (q - lag) % QUARTERS
+
         for q in range(QUARTERS):
 
             @pl.when(p + AHEAD < PANELS)
@@ -235,27 +240,25 @@
                     wait_load(p + AHEAD)
                 first_send(p + AHEAD, q)
 
-            for back, stage in ((0, stage_a), (1, stage_b), (2, stage_c), (3, stage_d)):
-                behind, at_q = (0, q - back) if q >= back else (1, q - back + QUARTERS)
-                when = (p < PANELS) if behind == 0 else (p > 0)
-                pl.when(when)(lambda: stage(p - behind, at_q))
-
-            n = p - 1
-
-            @pl.when(p > 0)
+            for lag, stage in zip(LAGS, (stage_a, stage_b, stage_c, stage_d)):
+                m, at_q = behind(q, lag)
+                pl.when((m >= 0) & (m < PANELS))(lambda: stage(m, at_q))
+
+            n, at_q = behind(q, LAGS[-1])
+
+            @pl.when((n >= 0) & (n < PANELS))
             def _():
-                stage_e(n, q)
-                if q == 0:
-                    pl.when(n > 1)(lambda: update(n - 2))
-                absorb(n, q)
-                if q == 1:
+                stage_e(n, at_q)
+                pl.when(n > 1)(lambda: update_rows(n - 2, at_q))
+                absorb(n, at_q)
+                if at_q == 1:
                     pl.when(n > 0)(lambda: scale(n - 1))
-                if q == QUARTERS - 1:
+                if at_q == QUARTERS - 1:
                     finish(n)
 
         return carry
 
-    lax.fori_loop(0, PANELS + 1, panel, 0)
+    lax.fori_loop(0, PANELS + -(-LAGS[-1] // QUARTERS), panel, 0)
 
     update(PANELS - 2)
     scale(PANELS - 1)
@@ -272,32 +275,24 @@
 
     lax.fori_loop(0, PANELS, close, 0)
 
-    def close_out(i, carry):
-        write(i).wait()
-        return carry
-
-    lax.fori_loop(0, ROWS // BLOCK, close_out, 0)
-
 
 def local(eigvecs, v_panels, t_panels):
     dma = pltpu.SemaphoreType.DMA
     anywhere = pl.BlockSpec(memory_space=pl.ANY)
     return pl.pallas_call(
         kernel,
-        out_shape=jax.ShapeDtypeStruct((ROWS, COLS), F32),
+        out_shape=pltpu.VMEM((ROWS, COLS), F32),
         in_specs=[anywhere] * 3,
-        out_specs=anywhere,
+        out_specs=pl.BlockSpec(memory_space=pltpu.VMEM),
         scratch_shapes=[
             pltpu.VMEM((PANELS, 2, SIDE, SIDE, STRIPE, LANES), F32),
-            pltpu.VMEM((ROWS, COLS), F32),
             pltpu.VMEM((ROWS, COLS), BF16),
             pltpu.VMEM((ROWS, COLS), BF16),
             pltpu.VMEM((WIDTH, CHUNK), BF16),
             pltpu.VMEM((WIDTH, CHUNK), BF16),
             pltpu.VMEM((2, ROWS, WIDTH), BF16),
             pltpu.VMEM((2, ROWS, WIDTH), BF16),
-            pltpu.VMEM((WIDTH, COLS), F32),
-            pltpu.VMEM((WIDTH, WIDTH), F32),
+            pltpu.VMEM((WIDTH, COLS + WIDTH), F32),
             pltpu.VMEM((PANELS, COLS, WIDTH), F32),
             pltpu.VMEM((PANELS, 3, COLS // 4, WIDTH), F32),
             pltpu.VMEM((PANELS, COLS, WIDTH), F32),
@@ -305,7 +300,6 @@
             pltpu.VMEM((WIDTH, COLS), BF16),
             dma((PANELS, 2)),
             dma,
-            dma((ROWS // BLOCK,)),
             dma((PANELS, QUARTERS, 2)),
             dma((PANELS, QUARTERS, 2)),
             dma((PANELS, QUARTERS, 2)),
@@ -320,7 +314,7 @@
             dma((PANELS,)),
         ],
         compiler_params=pltpu.CompilerParams(
-            collective_id=0, has_side_effects=True, vmem_limit_bytes=67043328
+            collective_id=0, has_side_effects=True, vmem_limit_bytes=58 * 2**20
         ),
     )(eigvecs, jnp.swapaxes(v_panels, 1, 2), jnp.swapaxes(t_panels, 1, 2))
 

time: 171 us -> 134 us (0.78)
  Pallas kernels: 167 us -> 132 us
  local copies, waits for them, and re-layouts: 4.47 us -> 2.02 us
    pallas_call x1, Pallas kernels: 167 us -> 132 us  [local(): pl.pallas_call(kernel, out_shape=pltpu.VMEM((ROWS, COLS), F32), in_specs=...]
    unnamed x1, local copies, waits for them, and re-layouts: 4.47 us -> 2.02 us
where the time goes in v2:
time: 134 us
  Pallas kernels  132 us (99%)
  local copies, waits for them, and re-layouts  2.02 us (2%)
    pallas_call x1, Pallas kernels, local(): pl.pallas_call(kernel, out_shape=pltpu.VMEM((ROWS, COLS), F32), in_specs=...  132 us

profile of v2, /device:TPU:0, one launch (start us, length us, event | category | flops | bytes accessed | tf_op | source)
XLA Modules:
  0.0 134.2 jit_solution(12436994495620046815)
XLA Ops:
  0.0 132.2 %shard_map.37 = f32[4096,256]{1,0:T(8,128)S(1)} custom-call(f32[4096,256]{1,0:T(8,128)} %z_in.1, f32[8,8,4096]{2,1,0:T(8,128)} %bitcast.2, f32[8,8,256]{2,1,0:T(8,128)} %bitcast.3), custom_call_target="tpu_custom_call" | custom-call | tf_op jit(solution)/shard_map/pallas_call | solution.py:282
  132.2 2.0 %copy.5 = f32[4096,256]{1,0:T(8,128)} copy(f32[4096,256]{1,0:T(8,128)S(1)} %shard_map.37) | data formatting | bytes 8388608

commit v3 on v2

--- a/solution.py
+++ b/solution.py
@@ -13,9 +13,10 @@
 CHUNK = 1024
 SPANS = ((0, 1024), (1024, 1024), (2048, 1024), (3072, 1280))
 QUARTERS = len(SPANS)
-BLOCK = 512
-AHEAD = 2
-LAGS = (0, 2, 4, 6, 8)
+BLOCK = 1024
+AHEAD = 3
+EARLY = 1
+LAGS = (0, 2, 4, 6, 7)
 
 
 def halves(x):
@@ -31,7 +32,7 @@
 
 def kernel(
     z_in, v_in, t_in, z,
-    vbuf, zh, zl, vh, vl, vnh, vnl, both, psend, prec, sfull, sh, sl,
+    vbuf, zh, zl, vh, vl, vnh, vnl, both, psend, prec, sfull, sh, sl, th, tl,
     load_sem, z_sem,
     near_sem, half_sem, row_sem, rowhalf_sem, core_sem, sent1, sent2, sent3,
     rs_sem, rs_sent, ag_sem, ag_sent,
@@ -143,13 +144,16 @@
         part = dot3((vh[...], vl[...]), right)
         both[...] = part if q == 0 else both[...] + part
 
-    quarter = COLS // 4
-    own_rows = pl.ds(pl.multiple_of(quarter * row, quarter), quarter)
+    share = COLS // (2 * SIDE)
+
+    def rows_of(wave, z_of):
+        start = pl.multiple_of(wave * (COLS // 2) + share * z_of, share)
+        return pl.ds(start, share)
 
     def take_s(n):
-        for d in (1, 2, 3):
-            rows = pl.ds(pl.multiple_of(quarter * wrap(row - d), quarter), quarter)
-            arrived(sfull.at[n, rows], ag_sem.at[n, d - 1])
+        for wave in (0, 1):
+            for d in (1, 2, 3):
+                arrived(sfull.at[n, rows_of(wave, wrap(row - d))], ag_sem.at[n, wave, d - 1])
         sh[...], sl[...] = halves(sfull[n].T)
 
     def finish(n):
@@ -162,20 +166,22 @@
             take_s(n - 1)
             psend[n] = (both[:, :COLS] - dot3(halves(both[:, COLS:]), (sh[...], sl[...]))).T
 
-        for d in (1, 2, 3):
-            rows = pl.ds(pl.multiple_of(quarter * wrap(row + d), quarter), quarter)
-            copy(psend.at[n, rows], prec.at[n, d - 1], rs_sent.at[n], rs_sem.at[n, d - 1], lifts[d - 1]).start()
+        for wave in (0, 1):
+            for d in (2, 1, 3):
+                src, dst = psend.at[n, rows_of(wave, wrap(row + d))], prec.at[n, wave, d - 1]
+                copy(src, dst, rs_sent.at[n], rs_sem.at[n, wave, d - 1], lifts[d - 1]).start()
 
     def scale(n):
-        total = psend[n, own_rows, :]
-        for d in (1, 2, 3):
-            arrived(prec.at[n, d - 1], rs_sem.at[n, d - 1])
-        for d in (1, 2, 3):
-            total = total + prec[n, d - 1]
         factor = jnp.concatenate([pair(n, i, ROWS, WIDTH) for i in range(SIDE * SIDE)], axis=0)
-        sfull[n, own_rows, :] = dot3(halves(total), halves(factor))
-        for d in (1, 2, 3):
-            push(sfull.at[n, own_rows], ag_sent.at[n], ag_sem.at[n, d - 1], lifts[d - 1])
+        th[...], tl[...] = halves(factor)
+        for wave in (0, 1):
+            own = rows_of(wave, row)
+            for d in (1, 3, 2):
+                arrived(prec.at[n, wave, d - 1], rs_sem.at[n, wave, d - 1])
+            total = psend[n, own, :] + prec[n, wave, 0] + prec[n, wave, 1] + prec[n, wave, 2]
+            sfull[n, own, :] = dot3(halves(total), (th[...], tl[...]))
+            for d in (2, 1, 3):
+                push(sfull.at[n, own], ag_sent.at[n], ag_sem.at[n, wave, d - 1], lifts[d - 1])
 
     def update_rows(n, q):
         slot, rows = lax.rem(n, 2), pl.ds(CHUNK * q, CHUNK)
@@ -196,6 +202,31 @@
 
         lax.fori_loop(0, ROWS // BLOCK, body, 0)
 
+    def near_chunk(m, q):
+        @pl.when(m < PANELS)
+        def _():
+            if q == 0:
+                wait_load(m)
+            first_send(m, q)
+
+    def near(p, q):
+        at = lambda chunk: (chunk // QUARTERS, chunk % QUARTERS)
+        if EARLY == 0:
+            m, at_q = at(AHEAD + q)
+            near_chunk(p + m, at_q)
+            return
+
+        @pl.when(p < EARLY)
+        def _():
+            for extra in (0, 1):
+                m, at_q = at(AHEAD + 2 * q + extra)
+                near_chunk(2 * p + m, at_q)
+
+        @pl.when(p >= EARLY)
+        def _():
+            m, at_q = at(AHEAD + QUARTERS * EARLY + q)
+            near_chunk(p + m, at_q)
+
     z_load = pltpu.make_async_copy(z_in, z, z_sem)
 
     def start_load(n, carry):
@@ -212,13 +243,8 @@
         pl.semaphore_signal(barrier, inc=1, device_id=device, device_id_type=MESH)
     pl.semaphore_wait(barrier, len(greeted))
 
-    def open_sends(n, carry):
-        wait_load(n)
-        for q in range(QUARTERS):
-            first_send(n, q)
-        return carry
-
-    lax.fori_loop(0, AHEAD, open_sends, 0)
+    for chunk in range(AHEAD):
+        near_chunk(jnp.int32(chunk // QUARTERS), chunk % QUARTERS)
     z_load.wait()
 
     def split_z(i, carry):
@@ -234,27 +260,32 @@
 
         for q in range(QUARTERS):
 
-            @pl.when(p + AHEAD < PANELS)
-            def _():
-                if q == 0:
-                    wait_load(p + AHEAD)
-                first_send(p + AHEAD, q)
-
-            for lag, stage in zip(LAGS, (stage_a, stage_b, stage_c, stage_d)):
-                m, at_q = behind(q, lag)
-                pl.when((m >= 0) & (m < PANELS))(lambda: stage(m, at_q))
-
-            n, at_q = behind(q, LAGS[-1])
-
-            @pl.when((n >= 0) & (n < PANELS))
-            def _():
-                stage_e(n, at_q)
-                pl.when(n > 1)(lambda: update_rows(n - 2, at_q))
-                absorb(n, at_q)
-                if at_q == 1:
+            near(p, q)
+
+            def run(stages):
+                for lag, stage in stages:
+                    m, at_q = behind(q, lag)
+                    pl.when((m >= 0) & (m < PANELS))(lambda: stage(m, at_q))
+
+            n, e_q = behind(q, LAGS[-1])
+            live = (n >= 0) & (n < PANELS)
+
+            def renew():
+                pl.when(n > 1)(lambda: update_rows(n - 2, e_q))
+
+            def work():
+                stage_e(n, e_q)
+                absorb(n, e_q)
+                if e_q == 1:
                     pl.when(n > 0)(lambda: scale(n - 1))
-                if at_q == QUARTERS - 1:
+                if e_q == QUARTERS - 1:
                     finish(n)
+
+            A, B, C, D = zip(LAGS, (stage_a, stage_b, stage_c, stage_d))
+            run((A, B))
+            pl.when(live)(renew)
+            run((C, D))
+            pl.when(live)(work)
 
         return carry
 
@@ -294,10 +325,12 @@
             pltpu.VMEM((2, ROWS, WIDTH), BF16),
             pltpu.VMEM((WIDTH, COLS + WIDTH), F32),
             pltpu.VMEM((PANELS, COLS, WIDTH), F32),
-            pltpu.VMEM((PANELS, 3, COLS // 4, WIDTH), F32),
+            pltpu.VMEM((PANELS, 2, 3, COLS // 8, WIDTH), F32),
             pltpu.VMEM((PANELS, COLS, WIDTH), F32),
             pltpu.VMEM((WIDTH, COLS), BF16),
             pltpu.VMEM((WIDTH, COLS), BF16),
+            pltpu.VMEM((WIDTH, WIDTH), BF16),
+            pltpu.VMEM((WIDTH, WIDTH), BF16),
             dma((PANELS, 2)),
             dma,
             dma((PANELS, QUARTERS, 2)),
@@ -308,9 +341,9 @@
             dma((PANELS,)),
             dma((PANELS,)),
             dma((PANELS,)),
-            dma((PANELS, 3)),
-            dma((PANELS,)),
-            dma((PANELS, 3)),
+            dma((PANELS, 2, 3)),
+            dma((PANELS,)),
+            dma((PANELS, 2, 3)),
             dma((PANELS,)),
         ],
         compiler_params=pltpu.CompilerParams(

time: 134 us -> 126 us (0.940)
  Pallas kernels: 132 us -> 124 us
    pallas_call x1, Pallas kernels: 132 us -> 124 us  [local(): pl.pallas_call(kernel, out_shape=pltpu.VMEM((ROWS, COLS), F32), in_specs=...]
where the time goes in v3:
time: 126 us
  Pallas kernels  124 us (98%)
  local copies, waits for them, and re-layouts  2.02 us (2%)
    pallas_call x1, Pallas kernels, local(): pl.pallas_call(kernel, out_shape=pltpu.VMEM((ROWS, COLS), F32), in_specs=...  124 us

profile of v3, /device:TPU:0, one launch (start us, length us, event | category | flops | bytes accessed | tf_op | source)
XLA Modules:
  0.0 126.1 jit_solution(2670039761119674286)
XLA Ops:
  0.0 124.1 %shard_map.37 = f32[4096,256]{1,0:T(8,128)S(1)} custom-call(f32[4096,256]{1,0:T(8,128)} %z_in.1, f32[8,8,4096]{2,1,0:T(8,128)} %bitcast.2, f32[8,8,256]{2,1,0:T(8,128)} %bitcast.3), custom_call_target="tpu_custom_call" | custom-call | tf_op jit(solution)/shard_map/pallas_call | solution.py:313
  124.1 2.0 %copy.5 = f32[4096,256]{1,0:T(8,128)} copy(f32[4096,256]{1,0:T(8,128)S(1)} %shard_map.37) | data formatting | bytes 8388608

commit v4 on v3

--- a/solution.py
+++ b/solution.py
@@ -9,11 +9,12 @@
 F32, BF16 = jnp.float32, jnp.bfloat16
 PANELS, WIDTH, ROWS, COLS = 8, 256, 4096, 256
 SIDE, STRIPE = 4, 8
-LANES = ROWS + WIDTH
+HALF = WIDTH // 2
 CHUNK = 1024
-SPANS = ((0, 1024), (1024, 1024), (2048, 1024), (3072, 1280))
+SPANS = ((0, 1024), (1024, 1024), (2048, 1024), (3072, 1024))
 QUARTERS = len(SPANS)
 BLOCK = 1024
+PIECES = 4
 AHEAD = 3
 EARLY = 1
 LAGS = (0, 2, 4, 6, 7)
@@ -32,8 +33,8 @@
 
 def kernel(
     z_in, v_in, t_in, z,
-    vbuf, zh, zl, vh, vl, vnh, vnl, both, psend, prec, sfull, sh, sl, th, tl,
-    load_sem, z_sem,
+    vbuf, tbuf, tall, zh, zl, vh, vl, vnh, vnl, both, psend, prec, sfull, sh, sl, th, tl,
+    load_sem, z_sem, tload_sem, t_sem, t_sent, lift_sem, liftpart_sem, swap_sem, lift_sent, swap_sent,
     near_sem, half_sem, row_sem, rowhalf_sem, core_sem, sent1, sent2, sent3,
     rs_sem, rs_sent, ag_sem, ag_sent,
 ):
@@ -66,62 +67,120 @@
     def gone(ref, send):
         copy(ref, ref, send, core_sem.at[0, 0], partner).wait_send()
 
-    def stripe(n, q, a_of, part=None):
-        start, size = SPANS[q]
-        if part is not None:
-            size //= 2
-            start += part * size
-        return vbuf.at[n, core, b, a_of, :, pl.ds(start, size)]
-
-    def line(n, q, b_of, part=None):
-        start, size = SPANS[q]
-        first, count = (0, SIDE) if part is None else (2 * part, 2)
-        return vbuf.at[n, core, b_of, pl.ds(first, count), :, pl.ds(start, size)]
+    class Vectors:
+        def __init__(self, n, q):
+            self.n, self.span = n, SPANS[q]
+            self.near = [near_sem.at[n, q, i] for i in (0, 1)]
+            self.half = [half_sem.at[n, q, i] for i in (0, 1)]
+            self.row = [row_sem.at[n, q, i] for i in (0, 1)]
+            self.rowhalf = [rowhalf_sem.at[n, q, i] for i in (0, 1)]
+            self.core, self.sent = core_sem.at[n, q], (sent1.at[n], sent2.at[n], sent3.at[n])
+
+        def stripe(self, a_of, part=None):
+            start, size = self.span
+            if part is not None:
+                size //= 2
+                start += part * size
+            return vbuf.at[self.n, core, b, a_of, :, pl.ds(start, size)]
+
+        def line(self, b_of, part=None):
+            first, count = (0, SIDE) if part is None else (2 * part, 2)
+            return vbuf.at[self.n, core, b_of, pl.ds(first, count), :, pl.ds(*self.span)]
+
+        def theirs(self):
+            return vbuf.at[self.n, 1 - core, :, :, :, pl.ds(*self.span)]
+
+    class Factors:
+        near, half, row, rowhalf = [[t_sem.at[2 * j + i] for i in (0, 1)] for j in range(4)]
+        core, sent = t_sem.at[8], (t_sent.at[0], t_sent.at[1], t_sent.at[2])
+
+        def stripe(self, a_of, part=None):
+            return tbuf.at[core, b, a_of, pl.ds(0, 2) if part is None else pl.ds(part, 1)]
+
+        def line(self, b_of, part=None):
+            first, count = (0, SIDE) if part is None else (2 * part, 2)
+            return tbuf.at[core, b_of, pl.ds(first, count)]
+
+        def theirs(self):
+            return tbuf.at[1 - core]
+
+    factors = Factors()
 
     def load(n):
-        own = lambda start, size: vbuf.at[n, core, b, a, :, pl.ds(start, size)]
-        return (
-            pltpu.make_async_copy(v_in.at[PANELS - 1 - n], own(0, ROWS), load_sem.at[n, 0]),
-            pltpu.make_async_copy(t_in.at[PANELS - 1 - n], own(ROWS, WIDTH), load_sem.at[n, 1]),
-        )
+        return (pltpu.make_async_copy(v_in.at[PANELS - 1 - n], vbuf.at[n, core, b, a], load_sem.at[n]),)
+
+    def load_t(g):
+        return pltpu.make_async_copy(t_in.at[PANELS - 1 - SIDE * g - row], tbuf.at[core, b, a, g], tload_sem.at[g])
 
     def wait_load(n):
         for one in load(n):
             one.wait()
 
-    def first_send(n, q):
-        push(stripe(n, q, a), sent1.at[n], near_sem.at[n, q, 0], up_a)
-        push(stripe(n, q, a), sent1.at[n], near_sem.at[n, q, 1], down_a)
-
-    def stage_a(n, q):
-        arrived(stripe(n, q, a_prev), near_sem.at[n, q, 0])
-        push(stripe(n, q, a_prev, 0), sent1.at[n], half_sem.at[n, q, 0], up_a)
-        arrived(stripe(n, q, a_next), near_sem.at[n, q, 1])
-        push(stripe(n, q, a_next, 1), sent1.at[n], half_sem.at[n, q, 1], down_a)
-
-    def stage_b(n, q):
-        arrived(stripe(n, q, a_far, 0), half_sem.at[n, q, 0])
-        arrived(stripe(n, q, a_far, 1), half_sem.at[n, q, 1])
-        push(line(n, q, b), sent2.at[n], row_sem.at[n, q, 0], up_b)
-        push(line(n, q, b), sent2.at[n], row_sem.at[n, q, 1], down_b)
-        push(line(n, q, b), sent3.at[n], core_sem.at[n, q], partner)
-
-    def stage_c(n, q):
-        arrived(line(n, q, b_prev), row_sem.at[n, q, 0])
-        push(line(n, q, b_prev, 0), sent2.at[n], rowhalf_sem.at[n, q, 0], up_b)
-        push(line(n, q, b_prev), sent3.at[n], core_sem.at[n, q], partner)
-        arrived(line(n, q, b_next), row_sem.at[n, q, 1])
-        push(line(n, q, b_next, 1), sent2.at[n], rowhalf_sem.at[n, q, 1], down_b)
-        push(line(n, q, b_next), sent3.at[n], core_sem.at[n, q], partner)
-
-    def stage_d(n, q):
-        arrived(line(n, q, b_far, 0), rowhalf_sem.at[n, q, 0])
-        arrived(line(n, q, b_far, 1), rowhalf_sem.at[n, q, 1])
-        push(line(n, q, b_far), sent3.at[n], core_sem.at[n, q], partner)
-
-    def stage_e(n, q):
-        start, size = SPANS[q]
-        arrived(vbuf.at[n, 1 - core, :, :, :, pl.ds(start, size)], core_sem.at[n, q])
+    def first_send(s):
+        push(s.stripe(a), s.sent[0], s.near[0], up_a)
+        push(s.stripe(a), s.sent[0], s.near[1], down_a)
+
+    def stage_a(s):
+        arrived(s.stripe(a_prev), s.near[0])
+        push(s.stripe(a_prev, 0), s.sent[0], s.half[0], up_a)
+        arrived(s.stripe(a_next), s.near[1])
+        push(s.stripe(a_next, 1), s.sent[0], s.half[1], down_a)
+
+    def stage_b(s):
+        arrived(s.stripe(a_far, 0), s.half[0])
+        arrived(s.stripe(a_far, 1), s.half[1])
+        push(s.line(b), s.sent[1], s.row[0], up_b)
+        push(s.line(b), s.sent[1], s.row[1], down_b)
+        push(s.line(b), s.sent[2], s.core, partner)
+
+    def stage_c(s):
+        arrived(s.line(b_prev), s.row[0])
+        push(s.line(b_prev, 0), s.sent[1], s.rowhalf[0], up_b)
+        push(s.line(b_prev), s.sent[2], s.core, partner)
+        arrived(s.line(b_next), s.row[1])
+        push(s.line(b_next, 1), s.sent[1], s.rowhalf[1], down_b)
+        push(s.line(b_next), s.sent[2], s.core, partner)
+
+    def stage_d(s):
+        arrived(s.line(b_far, 0), s.rowhalf[0])
+        arrived(s.line(b_far, 1), s.rowhalf[1])
+        push(s.line(b_far), s.sent[2], s.core, partner)
+
+    def stage_e(s):
+        arrived(s.theirs(), s.core)
+
+    def mine(g, z_of, of_core, piece=None):
+        rows = HALF if piece is None else HALF // PIECES
+        start = of_core * HALF + (0 if piece is None else piece * rows)
+        return tall.at[SIDE * g + z_of, pl.ds(pl.multiple_of(start, rows), rows)]
+
+    def lift_early():
+        stage_e(factors)
+        for g in (0, 1):
+            for i in range(SIDE * SIDE):
+                yy, xx = divmod(i, SIDE)
+                both_cores = jnp.concatenate([tbuf[0, yy, xx, g], tbuf[1, xx, yy, g]], axis=0)
+                tall[SIDE * g + row, pl.ds(2 * STRIPE * i, 2 * STRIPE), :] = both_cores
+        for d in (2, 1, 3):
+            push(mine(0, row, core), lift_sent.at[0], lift_sem.at[d - 1], lifts[d - 1])
+
+    def lift_late(piece):
+        for d in (2, 1, 3):
+            push(mine(1, row, core, piece), lift_sent.at[1], liftpart_sem.at[piece, d - 1], lifts[d - 1])
+
+    def swap(g):
+        for d in (1, 2, 3):
+            z_of = wrap(row - d)
+            if g == 0:
+                arrived(mine(0, z_of, core), lift_sem.at[d - 1])
+            else:
+                for piece in range(PIECES):
+                    arrived(mine(1, z_of, core, piece), liftpart_sem.at[piece, d - 1])
+            push(mine(g, z_of, core), swap_sent.at[g], swap_sem.at[g, d - 1], partner)
+
+    def swapped(g):
+        for d in (1, 2, 3):
+            arrived(mine(g, wrap(row - d), 1 - core), swap_sem.at[g, d - 1])
 
     def pair(n, i, start, size):
         yy, xx = divmod(i, SIDE)
@@ -172,8 +231,9 @@
                 copy(src, dst, rs_sent.at[n], rs_sem.at[n, wave, d - 1], lifts[d - 1]).start()
 
     def scale(n):
-        factor = jnp.concatenate([pair(n, i, ROWS, WIDTH) for i in range(SIDE * SIDE)], axis=0)
-        th[...], tl[...] = halves(factor)
+        pl.when(n == 0)(lambda: swapped(0))
+        pl.when(n == SIDE)(lambda: swapped(1))
+        th[...], tl[...] = halves(tall[n])
         for wave in (0, 1):
             own = rows_of(wave, row)
             for d in (1, 3, 2):
@@ -207,7 +267,7 @@
         def _():
             if q == 0:
                 wait_load(m)
-            first_send(m, q)
+            first_send(Vectors(m, q))
 
     def near(p, q):
         at = lambda chunk: (chunk // QUARTERS, chunk % QUARTERS)
@@ -234,6 +294,8 @@
             one.start()
         return carry
 
+    for g in (0, 1):
+        load_t(g).start()
     lax.fori_loop(0, PANELS, start_load, 0)
     z_load.start()
 
@@ -243,6 +305,9 @@
         pl.semaphore_signal(barrier, inc=1, device_id=device, device_id_type=MESH)
     pl.semaphore_wait(barrier, len(greeted))
 
+    for g in (0, 1):
+        load_t(g).wait()
+    first_send(factors)
     for chunk in range(AHEAD):
         near_chunk(jnp.int32(chunk // QUARTERS), chunk % QUARTERS)
     z_load.wait()
@@ -264,8 +329,10 @@
 
             def run(stages):
                 for lag, stage in stages:
+                    if lag % QUARTERS == q:
+                        pl.when(p == lag // QUARTERS)(lambda: stage(factors))
                     m, at_q = behind(q, lag)
-                    pl.when((m >= 0) & (m < PANELS))(lambda: stage(m, at_q))
+                    pl.when((m >= 0) & (m < PANELS))(lambda: stage(Vectors(m, at_q)))
 
             n, e_q = behind(q, LAGS[-1])
             live = (n >= 0) & (n < PANELS)
@@ -274,7 +341,7 @@
                 pl.when(n > 1)(lambda: update_rows(n - 2, e_q))
 
             def work():
-                stage_e(n, e_q)
+                stage_e(Vectors(n, e_q))
                 absorb(n, e_q)
                 if e_q == 1:
                     pl.when(n > 0)(lambda: scale(n - 1))
@@ -282,10 +349,18 @@
                     finish(n)
 
             A, B, C, D = zip(LAGS, (stage_a, stage_b, stage_c, stage_d))
-            run((A, B))
+            run((B, A))
             pl.when(live)(renew)
-            run((C, D))
+            run((D, C))
+            if q == LAGS[-1] % QUARTERS:
+                pl.when(p == LAGS[-1] // QUARTERS)(lift_early)
             pl.when(live)(work)
+            if q == 1:
+                for piece in range(PIECES):
+                    pl.when(p == 2 + piece)(lambda: lift_late(piece))
+            if q == QUARTERS - 1:
+                pl.when(p == 2)(lambda: swap(0))
+                pl.when(p == 6)(lambda: swap(1))
 
         return carry
 
@@ -305,6 +380,12 @@
         return carry
 
     lax.fori_loop(0, PANELS, close, 0)
+    gone(tbuf.at[0, 0, pl.ds(0, 3)], t_sent.at[0])
+    gone(tbuf.at[0, pl.ds(0, 3)], t_sent.at[1])
+    gone(tbuf.at[0], t_sent.at[2])
+    for g in (0, 1):
+        gone(tall.at[pl.ds(0, 3), pl.ds(0, HALF)], lift_sent.at[g])
+        gone(tall.at[pl.ds(0, 3), pl.ds(0, HALF)], swap_sent.at[g])
 
 
 def local(eigvecs, v_panels, t_panels):
@@ -316,7 +397,9 @@
         in_specs=[anywhere] * 3,
         out_specs=pl.BlockSpec(memory_space=pltpu.VMEM),
         scratch_shapes=[
-            pltpu.VMEM((PANELS, 2, SIDE, SIDE, STRIPE, LANES), F32),
+            pltpu.VMEM((PANELS, 2, SIDE, SIDE, STRIPE, ROWS), F32),
+            pltpu.VMEM((2, SIDE, SIDE, 2, STRIPE, WIDTH), F32),
+            pltpu.VMEM((PANELS, WIDTH, WIDTH), F32),
             pltpu.VMEM((ROWS, COLS), BF16),
             pltpu.VMEM((ROWS, COLS), BF16),
             pltpu.VMEM((WIDTH, CHUNK), BF16),
@@ -331,8 +414,16 @@
             pltpu.VMEM((WIDTH, COLS), BF16),
             pltpu.VMEM((WIDTH, WIDTH), BF16),
             pltpu.VMEM((WIDTH, WIDTH), BF16),
-            dma((PANELS, 2)),
+            dma((PANELS,)),
             dma,
+            dma((2,)),
+            dma((9,)),
+            dma((3,)),
+            dma((3,)),
+            dma((PIECES, 3)),
+            dma((2, 3)),
+            dma((2,)),
+            dma((2,)),
             dma((PANELS, QUARTERS, 2)),
             dma((PANELS, QUARTERS, 2)),
             dma((PANELS, QUARTERS, 2)),

time: 126 us -> 123 us (0.976)
  Pallas kernels: 124 us -> 121 us
    pallas_call x1, Pallas kernels: 124 us -> 121 us  [local(): pl.pallas_call(kernel, out_shape=pltpu.VMEM((ROWS, COLS), F32), in_specs=...]
where the time goes in v4:
time: 123 us
  Pallas kernels  121 us (98%)
  local copies, waits for them, and re-layouts  2.02 us (2%)
    pallas_call x1, Pallas kernels, local(): pl.pallas_call(kernel, out_shape=pltpu.VMEM((ROWS, COLS), F32), in_specs=...  121 us

profile of v4, /device:TPU:0, one launch (start us, length us, event | category | flops | bytes accessed | tf_op | source)
XLA Modules:
  0.0 123.0 jit_solution(1953282018887212255)
XLA Ops:
  0.0 121.0 %shard_map.37 = f32[4096,256]{1,0:T(8,128)S(1)} custom-call(f32[4096,256]{1,0:T(8,128)} %z_in.1, f32[8,8,4096]{2,1,0:T(8,128)} %bitcast.2, f32[8,8,256]{2,1,0:T(8,128)} %bitcast.3), custom_call_target="tpu_custom_call" | custom-call | tf_op jit(solution)/shard_map/pallas_call | solution.py:394
  121.0 2.0 %copy.5 = f32[4096,256]{1,0:T(8,128)} copy(f32[4096,256]{1,0:T(8,128)S(1)} %shard_map.37) | data formatting | bytes 8388608

commit v5 on v4

--- a/solution.py
+++ b/solution.py
@@ -15,6 +15,7 @@
 QUARTERS = len(SPANS)
 BLOCK = 1024
 PIECES = 4
+BAND = 1024
 AHEAD = 3
 EARLY = 1
 LAGS = (0, 2, 4, 6, 7)
@@ -32,8 +33,8 @@
 
 
 def kernel(
-    z_in, v_in, t_in, z,
-    vbuf, tbuf, tall, zh, zl, vh, vl, vnh, vnl, both, psend, prec, sfull, sh, sl, th, tl,
+    z_in, v_in, t_in, z, vnh, vnl, sh, sl,
+    vbuf, tbuf, tall, zh, zl, vh, vl, both, psend, prec, sfull, th, tl,
     load_sem, z_sem, tload_sem, t_sem, t_sent, lift_sem, liftpart_sem, swap_sem, lift_sent, swap_sent,
     near_sem, half_sem, row_sem, rowhalf_sem, core_sem, sent1, sent2, sent3,
     rs_sem, rs_sent, ag_sem, ag_sent,
@@ -369,7 +370,6 @@
     update(PANELS - 2)
     scale(PANELS - 1)
     take_s(PANELS - 1)
-    update(PANELS - 1, last=True)
 
     def close(n, carry):
         gone(vbuf.at[n, 0, 0, pl.ds(0, 3)], sent1.at[n])
@@ -388,14 +388,26 @@
         gone(tall.at[pl.ds(0, 3), pl.ds(0, HALF)], swap_sent.at[g])
 
 
+def last_update(z, vnh, vnl, sh, sl, out):
+    rows = pl.ds(pl.multiple_of(pl.program_id(0) * BAND, BAND), BAND)
+    slot = (PANELS - 1) % 2
+    out[...] = z[rows, :] - dot3((vnh[slot, rows, :], vnl[slot, rows, :]), (sh[...], sl[...]))
+
+
 def local(eigvecs, v_panels, t_panels):
     dma = pltpu.SemaphoreType.DMA
     anywhere = pl.BlockSpec(memory_space=pl.ANY)
-    return pl.pallas_call(
+    state = pl.pallas_call(
         kernel,
-        out_shape=pltpu.VMEM((ROWS, COLS), F32),
+        out_shape=(
+            pltpu.VMEM((ROWS, COLS), F32),
+            pltpu.VMEM((2, ROWS, WIDTH), BF16),
+            pltpu.VMEM((2, ROWS, WIDTH), BF16),
+            pltpu.VMEM((WIDTH, COLS), BF16),
+            pltpu.VMEM((WIDTH, COLS), BF16),
+        ),
         in_specs=[anywhere] * 3,
-        out_specs=pl.BlockSpec(memory_space=pltpu.VMEM),
+        out_specs=(pl.BlockSpec(memory_space=pltpu.VMEM),) * 5,
         scratch_shapes=[
             pltpu.VMEM((PANELS, 2, SIDE, SIDE, STRIPE, ROWS), F32),
             pltpu.VMEM((2, SIDE, SIDE, 2, STRIPE, WIDTH), F32),
@@ -404,14 +416,10 @@
             pltpu.VMEM((ROWS, COLS), BF16),
             pltpu.VMEM((WIDTH, CHUNK), BF16),
             pltpu.VMEM((WIDTH, CHUNK), BF16),
-            pltpu.VMEM((2, ROWS, WIDTH), BF16),
-            pltpu.VMEM((2, ROWS, WIDTH), BF16),
             pltpu.VMEM((WIDTH, COLS + WIDTH), F32),
             pltpu.VMEM((PANELS, COLS, WIDTH), F32),
             pltpu.VMEM((PANELS, 2, 3, COLS // 8, WIDTH), F32),
             pltpu.VMEM((PANELS, COLS, WIDTH), F32),
-            pltpu.VMEM((WIDTH, COLS), BF16),
-            pltpu.VMEM((WIDTH, COLS), BF16),
             pltpu.VMEM((WIDTH, WIDTH), BF16),
             pltpu.VMEM((WIDTH, WIDTH), BF16),
             dma((PANELS,)),
@@ -438,9 +446,17 @@
             dma((PANELS,)),
         ],
         compiler_params=pltpu.CompilerParams(
-            collective_id=0, has_side_effects=True, vmem_limit_bytes=58 * 2**20
+            collective_id=0, has_side_effects=True, vmem_limit_bytes=49 * 2**20
         ),
     )(eigvecs, jnp.swapaxes(v_panels, 1, 2), jnp.swapaxes(t_panels, 1, 2))
+    return pl.pallas_call(
+        last_update,
+        out_shape=jax.ShapeDtypeStruct((ROWS, COLS), F32),
+        grid=(ROWS // BAND,),
+        in_specs=[pl.BlockSpec(memory_space=pltpu.VMEM)] * 5,
+        out_specs=pl.BlockSpec((BAND, COLS), lambda i: (i, 0)),
+        compiler_params=pltpu.CompilerParams(vmem_limit_bytes=8 * 2**20),
+    )(*[pltpu.with_memory_space_constraint(one, pltpu.VMEM) for one in state])
 
 
 def solution(mesh):

time: 123 us -> 122 us (level)
  local copies, waits for them, and re-layouts: 2.02 us -> 0 us
    unnamed x1 -> x0, local copies, waits for them, and re-layouts: 2.02 us -> none
    pallas_call x1 -> x2, Pallas kernels: 121 us -> 122 us  [the longest x1 119 us: local(): pl.pallas_call(kernel, out_shape=(pltpu.VMEM((ROWS, COLS), F32), pltpu.VM...]
where the time goes in v5:
time: 122 us
  Pallas kernels  122 us (100%)
    pallas_call x1, Pallas kernels, local(): pl.pallas_call(kernel, out_shape=(pltpu.VMEM((ROWS, COLS), F32), pltpu.VM...  119 us
    pallas_call x1, Pallas kernels, local(): pl.pallas_call(last_update, out_shape=jax.ShapeDtypeStruct((ROWS, COLS),...  3.71 us

profile of v5, /device:TPU:0, one launch (start us, length us, event | category | flops | bytes accessed | tf_op | source)
XLA Modules:
  0.0 122.4 jit_solution(18224275235970887608)
XLA Ops:
  0.0 118.7 %shard_map.37 = (f32[4096,256]{1,0:T(8,128)S(1)}, bf16[2,4096,256]{2,1,0:T(8,128)(2,1)S(1)}, bf16[2,4096,256]{2,1,0:T(8,128)(2,1)S(1)}, bf16[256,256]{1,0:T(8,128)(2,1)S(1)}, bf16[256,256]{1,0:T(8,128)(2,1)S(1)}) custom-call(f32[4096,256]{1,0:T(8,128)} %z_in.1, f32[8,8,4096]{2,1,0:T(8,128)} %bitcast.2, f32[8,8,256]{2,1,0:T(8,128)} %bitcast.3), custom_call_target="tpu_custom_call" | custom-call | tf_op jit(solution)/shard_map/pallas_call | solution.py:400
  118.7 3.7 %shard_map.38 = f32[4096,256]{1,0:T(8,128)} custom-call(f32[4096,256]{1,0:T(8,128)S(1)} %get-tuple-element.10.z, bf16[2,4096,256]{2,1,0:T(8,128)(2,1)S(1)} %get-tuple-element.11.vnh, bf16[2,4096,256]{2,1,0:T(8,128)(2,1)S(1)} %get-tuple-element.12.vnl, bf16[256,256]{1,0:T(8,128)(2,1)S(1)} %get-tuple-element.13.sh, bf16[256,256]{1,0:T(8,128)(2,1)S(1)} %get-tuple-element.14.sl), custom_call_target="tpu_custom_call" | custom-call | tf_op jit(solution)/shard_map/pallas_call | solution.py:452
